TPU v7x, 256 devices: a whole 4x4x8 slice. The times are simulated.
256 devices in a mesh: dp: 64 (over z, y, core), mp: 4 (over x).
Axes of the slice: x: 4, y: 4, z: 8, core: 2. Of those that a mesh axis runs over, the one named last changes fastest.
Arguments:
- patches: bfloat16 [131072, 1024], P('dp'), may hold values from -110 to 110
- dest_owner: int32 [8192], P('dp'), may hold values from 0 to 63, as said below
- dest_slot: int32 [8192], P('dp'), may hold values from 0 to 127
- packed_image: int32 [8192], P('dp'), may hold values from -1 to 15, as said below
- w_query: bfloat16 [1024, 1024], P(None, 'mp'), may hold values from -0.328125 to 0.328125
- w_key: bfloat16 [1024, 1024], P(None, 'mp'), may hold values from -1.9375 to 1.9375
- w_value: bfloat16 [1024, 1024], P(None, 'mp'), may hold values from -0.1875 to 0.1875
- w_out: bfloat16 [1024, 1024], P('mp'), may hold values from -0.1875 to 0.1875
Outputs:
- packed_out: bfloat16 [131072, 1024], P('dp', 'mp')
- pooled_out: bfloat16 [1024, 1024], P('dp', 'mp')
Inputs may be any that keep to these rules, and one draw needn't show every extreme that they name: dest_owner and dest_slot take the tiles of all indices of dp one to one onto the 128 tile slots of every packed sequence; each index of dp holds exactly 2 tiles for each packed sequence. `packed_image`: in every packed sequence the images 0, 1, 2 and so on lie on consecutive tile slots from slot 0 in the order of their numbers, each on 8 to 16 slots; fewer than 16 slots stay empty after the last image and hold -1.
All inputs are finite; a program needn't handle non-finite values.
Results may differ from a plain program's by a relative error of at most 0.0075.
Values may be sent and summed in bfloat16 or wider, within the bound.
No kernel may reach another device: no remote copies, remote signals or barrier semaphores. Data moves between devices by JAX's collectives and lax.ppermute only.
A program may use at most 128 MiB of HBM per device.

v0:
```python
import jax
import jax.numpy as jnp
from jax import lax
from jax.sharding import PartitionSpec as P

HEAD_DIM = 64
IMG_OWN = 16
EPSILON = 1e-06


def cut_along(shard, dim, length):
    lengths = shard.shape
    tiles = shard.reshape(*lengths[:dim], length, lengths[dim] // length, *lengths[dim + 1 :])
    return jnp.moveaxis(tiles, dim, 0)


def sent_and_summed(shard, axis, dim):
    length = lax.axis_size(axis)
    tiles = lax.all_to_all(cut_along(shard, dim, length), axis, 0, 0, tiled=True)
    return jnp.sum(tiles.astype(jnp.float32), axis=0)


def sent_to_all(shard, axis):
    copies = jnp.broadcast_to(shard, (lax.axis_size(axis), *shard.shape))
    return lax.all_to_all(copies, axis, split_axis=0, concat_axis=0, tiled=True)


def of_everyone(shard, axis):
    return sent_to_all(shard, axis).sum(axis=0)


def in_one(arrays, axis):
    line, at, outs = (jnp.concatenate([a.reshape(-1) for a in arrays]), 0, [])
    running = of_everyone(line, axis)
    for a in arrays:
        outs.append(running[at : at + a.size].reshape(a.shape))
        at += a.size
    return tuple(outs)


def normalize(rows):
    values = rows.astype(jnp.float32)
    centred = values - jnp.mean(values, axis=-1, keepdims=True)
    spread = jnp.mean(centred * centred, axis=-1, keepdims=True)
    return (centred * lax.rsqrt(spread + EPSILON)).astype(jnp.bfloat16)


def attend(queries, key_rows, values, allowed, present):
    scores = jnp.einsum(
        "qhd,khd->hqk", queries, key_rows, preferred_element_type=jnp.float32
    ) * HEAD_DIM ** (-0.5)
    masked = jnp.where(allowed[None], scores, -1e30)
    peak = jnp.max(masked, axis=-1, keepdims=True)
    raised = jnp.where(allowed[None], jnp.exp(scores - peak), 0.0)
    denominator = jnp.sum(raised, axis=-1, keepdims=True)
    denominator = jnp.where(present[None, :, None], denominator, 1.0)
    weights = (raised / denominator).astype(jnp.bfloat16)
    return jnp.einsum("hqk,khd->qhd", weights, values, preferred_element_type=jnp.float32).astype(
        jnp.bfloat16
    )


def whole_rows(queries, key_rows, values, segment, present):
    count_rows = queries.shape[0]
    block_rows = min(512, count_rows)

    def one_block(step_index):
        first_row = step_index * block_rows
        query_part = lax.dynamic_slice_in_dim(queries, first_row, block_rows, 0)
        segment_part = lax.dynamic_slice_in_dim(segment, first_row, block_rows, 0)
        live_rows = lax.dynamic_slice_in_dim(present, first_row, block_rows, 0)
        allowed = (segment_part[:, None] == segment[None, :]) & live_rows[:, None]
        return attend(query_part, key_rows, values, allowed, live_rows)

    outcome = lax.map(one_block, jnp.arange(count_rows // block_rows, dtype=jnp.int32))
    return outcome.reshape(count_rows, -1)


def on_device(patches, dest_owner, dest_slot, packed_image, w_query, w_key, w_value, w_out):
    senders = lax.axis_size("dp")
    splits = lax.axis_size("mp")
    slot_count = dest_owner.shape[0]
    per_owner = slot_count // senders
    tile_size = patches.shape[0] // slot_count
    full_width = patches.shape[1]
    part_width = full_width // splits
    numbers = jnp.arange(slot_count, dtype=jnp.int32)
    same_owner = dest_owner[:, None] == dest_owner[None, :]
    ranking = jnp.sum(
        (same_owner & (numbers[None, :] < numbers[:, None])).astype(jnp.int32), axis=1
    )
    position = dest_owner * per_owner + ranking
    picked = position[None, :] == numbers[:, None]
    ordering = jnp.sum(jnp.where(picked, numbers[None, :], 0), axis=1)
    slot_sent = jnp.sum(jnp.where(picked, dest_slot[None, :], 0), axis=1)
    got_slot = lax.all_to_all(slot_sent, "dp", split_axis=0, concat_axis=0, tiled=True)
    arrive = jnp.sum(jnp.where(got_slot[None, :] == numbers[:, None], numbers[None, :], 0), axis=1)
    tile_data = patches.reshape(slot_count, tile_size, full_width)
    column_start = lax.axis_index("mp") * part_width
    own_part = lax.dynamic_slice_in_dim(tile_data, column_start, part_width, 2)
    outgoing = jnp.take(own_part, ordering, axis=0).reshape(slot_count * tile_size, part_width)
    incoming = lax.all_to_all(outgoing, "dp", split_axis=0, concat_axis=0, tiled=True)
    own_cols = jnp.take(
        incoming.reshape(slot_count, tile_size, part_width), arrive, axis=0
    ).reshape(slot_count * tile_size, part_width)
    full_rows = lax.all_gather(own_cols, "mp", axis=1, tiled=True)
    count_rows = slot_count * tile_size
    segment = jnp.repeat(packed_image, tile_size)
    present = segment >= 0
    normed = normalize(full_rows)
    head_count = w_query.shape[1] // HEAD_DIM
    queries = (
        jnp.dot(normed, w_query, preferred_element_type=jnp.float32)
        .astype(jnp.bfloat16)
        .reshape(count_rows, head_count, HEAD_DIM)
    )
    key_rows = (
        jnp.dot(normed, w_key, preferred_element_type=jnp.float32)
        .astype(jnp.bfloat16)
        .reshape(count_rows, head_count, HEAD_DIM)
    )
    values = (
        jnp.dot(normed, w_value, preferred_element_type=jnp.float32)
        .astype(jnp.bfloat16)
        .reshape(count_rows, head_count, HEAD_DIM)
    )
    attended = whole_rows(queries, key_rows, values, segment, present)
    head_term = jnp.dot(attended, w_out, preferred_element_type=jnp.float32)
    summed = sent_and_summed(head_term.astype(jnp.bfloat16), "mp", 1)
    result_rows = jnp.where(present[:, None], own_cols.astype(jnp.float32) + summed, 0.0)
    packed_out = result_rows.astype(jnp.bfloat16)
    labels = jnp.arange(IMG_OWN, dtype=jnp.int32)
    member = (segment[None, :] == labels[:, None]).astype(jnp.float32)
    sums = jnp.dot(member, result_rows)
    image_rows = jnp.sum(member, axis=1)
    filled = image_rows > 0
    pooled = sums / jnp.maximum(image_rows, 1.0)[:, None]
    local_sum = jnp.sum(jnp.where(filled[:, None], pooled, 0.0), axis=0)
    local_count = jnp.sum(filled.astype(jnp.float32))
    grand_total, number = in_one((local_sum, local_count), "dp")
    centre = grand_total / number
    pooled_out = jnp.where(filled[:, None], pooled - centre[None, :], 0.0).astype(jnp.bfloat16)
    return (packed_out, pooled_out)


def solution(mesh):
    in_specs = (
        P("dp", None),
        P("dp"),
        P("dp"),
        P("dp"),
        P(None, "mp"),
        P(None, "mp"),
        P(None, "mp"),
        P("mp", None),
    )
    out_specs = (P("dp", "mp"), P("dp", "mp"))
    return jax.shard_map(
        on_device, mesh=mesh, in_specs=in_specs, out_specs=out_specs, check_vma=False
    )
```

profile of v0, /device:TPU:1, one launch (start us, length us, event | category | flops | bytes accessed | tf_op | source)
XLA Modules:
  0.0 322.7 jit_solution(6817620751752851636)
XLA Ops:
  10.3 13.1 %all-to-all-start.1 = ((s32[64,2,1]{1,2,0:T(1,128)}), s32[64,2,1]{1,2,0:T(1,128)S(1)}, u32[]{:S(2)}, u32[]{:S(2)}) async-start(s32[64,2,1]{1,2,0:T(1,128)} %bitcast), calls=%async_computation.1 | async-start | bytes 65536 | tf_op jit(solution)/shard_map/all_to_all | solution.py:96
  26.6 6.2 %all-to-all-done.1 = s32[64,2,1]{1,2,0:T(1,128)S(1)} async-done(((s32[64,2,1]{1,2,0:T(1,128)}), s32[64,2,1]{1,2,0:T(1,128)S(1)}, u32[]{:S(2)}, u32[]{:S(2)}) %all-to-all-start.1) | async-done | bytes 544 | tf_op jit(solution)/shard_map/all_to_all | solution.py:96
  32.8 4.7 %all-to-all-start = ((bf16[64,32,256]{2,1,0:T(8,128)(2,1)}), bf16[64,32,256]{2,1,0:T(8,128)(2,1)S(1)}, u32[]{:S(2)}, u32[]{:S(2)}) async-start(bf16[64,32,256]{2,1,0:T(8,128)(2,1)} %bitcast.2), calls=%async_computation | async-start | bytes 2097152 | tf_op jit(solution)/shard_map/all_to_all | solution.py:102
  39.2 26.7 %all-to-all-done = bf16[64,32,256]{2,1,0:T(8,128)(2,1)S(1)} async-done(((bf16[64,32,256]{2,1,0:T(8,128)(2,1)}), bf16[64,32,256]{2,1,0:T(8,128)(2,1)S(1)}, u32[]{:S(2)}, u32[]{:S(2)}) %all-to-all-start) | async-done | bytes 1048608 | tf_op jit(solution)/shard_map/all_to_all | solution.py:102
  67.9 49.4 %all-gather.2.cloned.1.call-done = bf16[2048,1024]{1,0:T(8,128)(2,1)} async-done(((bf16[2048,256]{1,0:T(8,128)(2,1)}), bf16[2048,1024]{1,0:T(8,128)(2,1)}) %all-gather.2.cloned.1.call-update) | async-done | bytes 4194320 | tf_op jit(solution)/shard_map/all_gather | solution.py:106
  117.4 3.0 convert_reduce_fusion
  123.4 2.3 convolution_convert_fusion.3
  125.7 2.3 convolution_convert_fusion.2
  130.3 98.7 %while.11 = (s32[]{:T(128)}, bf16[4,512,4,64]{1,3,2,0:T(8,128)(2,1)S(1)}, s32[4]{0:T(128)S(1)}, s32[2048]{0:T(1024)S(1)}, pred[2048]{0:T(1024)(128)(4,1)S(1)}, /...) while((s32[]{:T(128)}, ...), condition=%wide.region_9.11_spmd.clone, body=%wide.region_6.0_spmd.clone.sunk | while | flops 1646399488 | bytes 40707776 | solution.py:75
  132.8 13.4 %fusion.69 = (f32[4,512]{1,0:T(4,128)S(1)}, f32[4,512,2048]{2,1,0:T(8,128)}) fusion(pred[512,2048]{1,0:T(8,128)(4,1)S(1)} %compare_and_fusion.4, bf16[2048,4,64]{0,2,1:T(8,128)(2,1)} %get-tuple-element.197, bf16[2048,4,64]{0,2,1:T(8,128)(2,1)} %get-tuple-element.196, s32[]{:T(128)S(6)} %select_n.104), kind=kOutput, calls=%fused_computation.75.clone.1 | convolution fusion | flops 1098909696 | bytes 21505024 | tf_op jit(solution)/shard_map/while/body/eval_jaxpr/sub | solution.py:54
  146.2 8.7 %fusion.70 = bf16[4,512,4,64]{1,3,2,0:T(8,128)(2,1)S(1)} fusion(bf16[4,512,4,64]{1,3,2,0:T(8,128)(2,1)S(1)} %get-tuple-element.179, s32[]{:T(128)} %get-tuple-element.178, bf16[2048,4,64]{0,2,1:T(8,128)(2,1)} %get-tuple-element.198, f32[4,512,2048]{2,1,0:T(8,128)} %get-tuple-element.163, f32[4,512]{1,0:T(4,128)S(1)} %broadcast_select_fusion.4), kind=kOutput, calls=%fused_computation.17.clone.1 | convolution fusion | flops 545390592 | bytes 18096132 | tf_op jit(solution)/shard_map/while/body/eval_jaxpr/hqk,khd->qhd/dot_general | solution.py:58
  157.4 13.4 %fusion.69 = (f32[4,512]{1,0:T(4,128)S(1)}, f32[4,512,2048]{2,1,0:T(8,128)}) fusion(pred[512,2048]{1,0:T(8,128)(4,1)S(1)} %compare_and_fusion.4, bf16[2048,4,64]{0,2,1:T(8,128)(2,1)} %get-tuple-element.197, bf16[2048,4,64]{0,2,1:T(8,128)(2,1)} %get-tuple-element.196, s32[]{:T(128)S(6)} %select_n.104), kind=kOutput, calls=%fused_computation.75.clone.1 | convolution fusion | flops 1098909696 | bytes 21505024 | tf_op jit(solution)/shard_map/while/body/eval_jaxpr/sub | solution.py:54
  170.9 8.7 %fusion.70 = bf16[4,512,4,64]{1,3,2,0:T(8,128)(2,1)S(1)} fusion(bf16[4,512,4,64]{1,3,2,0:T(8,128)(2,1)S(1)} %get-tuple-element.179, s32[]{:T(128)} %get-tuple-element.178, bf16[2048,4,64]{0,2,1:T(8,128)(2,1)} %get-tuple-element.198, f32[4,512,2048]{2,1,0:T(8,128)} %get-tuple-element.163, f32[4,512]{1,0:T(4,128)S(1)} %broadcast_select_fusion.4), kind=kOutput, calls=%fused_computation.17.clone.1 | convolution fusion | flops 545390592 | bytes 18096132 | tf_op jit(solution)/shard_map/while/body/eval_jaxpr/hqk,khd->qhd/dot_general | solution.py:58
  182.1 13.5 %fusion.69 = (f32[4,512]{1,0:T(4,128)S(1)}, f32[4,512,2048]{2,1,0:T(8,128)}) fusion(pred[512,2048]{1,0:T(8,128)(4,1)S(1)} %compare_and_fusion.4, bf16[2048,4,64]{0,2,1:T(8,128)(2,1)} %get-tuple-element.197, bf16[2048,4,64]{0,2,1:T(8,128)(2,1)} %get-tuple-element.196, s32[]{:T(128)S(6)} %select_n.104), kind=kOutput, calls=%fused_computation.75.clone.1 | convolution fusion | flops 1098909696 | bytes 21505024 | tf_op jit(solution)/shard_map/while/body/eval_jaxpr/sub | solution.py:54
  195.6 8.7 %fusion.70 = bf16[4,512,4,64]{1,3,2,0:T(8,128)(2,1)S(1)} fusion(bf16[4,512,4,64]{1,3,2,0:T(8,128)(2,1)S(1)} %get-tuple-element.179, s32[]{:T(128)} %get-tuple-element.178, bf16[2048,4,64]{0,2,1:T(8,128)(2,1)} %get-tuple-element.198, f32[4,512,2048]{2,1,0:T(8,128)} %get-tuple-element.163, f32[4,512]{1,0:T(4,128)S(1)} %broadcast_select_fusion.4), kind=kOutput, calls=%fused_computation.17.clone.1 | convolution fusion | flops 545390592 | bytes 18096132 | tf_op jit(solution)/shard_map/while/body/eval_jaxpr/hqk,khd->qhd/dot_general | solution.py:58
  206.8 13.4 %fusion.69 = (f32[4,512]{1,0:T(4,128)S(1)}, f32[4,512,2048]{2,1,0:T(8,128)}) fusion(pred[512,2048]{1,0:T(8,128)(4,1)S(1)} %compare_and_fusion.4, bf16[2048,4,64]{0,2,1:T(8,128)(2,1)} %get-tuple-element.197, bf16[2048,4,64]{0,2,1:T(8,128)(2,1)} %get-tuple-element.196, s32[]{:T(128)S(6)} %select_n.104), kind=kOutput, calls=%fused_computation.75.clone.1 | convolution fusion | flops 1098909696 | bytes 21505024 | tf_op jit(solution)/shard_map/while/body/eval_jaxpr/sub | solution.py:54
  220.2 8.7 %fusion.70 = bf16[4,512,4,64]{1,3,2,0:T(8,128)(2,1)S(1)} fusion(bf16[4,512,4,64]{1,3,2,0:T(8,128)(2,1)S(1)} %get-tuple-element.179, s32[]{:T(128)} %get-tuple-element.178, bf16[2048,4,64]{0,2,1:T(8,128)(2,1)} %get-tuple-element.198, f32[4,512,2048]{2,1,0:T(8,128)} %get-tuple-element.163, f32[4,512]{1,0:T(4,128)S(1)} %broadcast_select_fusion.4), kind=kOutput, calls=%fused_computation.17.clone.1 | convolution fusion | flops 545390592 | bytes 18096132 | tf_op jit(solution)/shard_map/while/body/eval_jaxpr/hqk,khd->qhd/dot_general | solution.py:58
  230.1 3.3 %convolution_convert_fusion = bf16[2048,1024]{0,1:T(8,128)(2,1)} fusion(bf16[2048,256]{0,1:T(8,128)(2,1)S(1)} %bitcast.50, bf16[256,1024]{1,0:T(8,128)(2,1)S(1)} %copy-done), kind=kOutput, calls=%fused_computation.33 | convolution fusion | flops 1075838976 | bytes 5767168 | tf_op jit(solution)/shard_map/dot_general | solution.py:128
  233.4 5.0 %all-to-all-start.2 = ((bf16[4,2048,256]{1,2,0:T(8,128)(2,1)}), bf16[4,2048,256]{1,2,0:T(8,128)(2,1)}, u32[]{:S(2)}, u32[]{:S(2)}) async-start(bf16[4,2048,256]{1,2,0:T(8,128)(2,1)} %bitcast.47), calls=%async_computation.2 | async-start | bytes 8388608 | tf_op jit(solution)/shard_map/all_to_all | solution.py:19
  240.5 44.8 %all-to-all-done.2 = bf16[4,2048,256]{1,2,0:T(8,128)(2,1)} async-done(((bf16[4,2048,256]{1,2,0:T(8,128)(2,1)}), bf16[4,2048,256]{1,2,0:T(8,128)(2,1)}, u32[]{:S(2)}, u32[]{:S(2)}) %all-to-all-start.2) | async-done | bytes 4194336 | tf_op jit(solution)/shard_map/all_to_all | solution.py:19
  285.3 3.2 %convert_reduce_fusion.1 = f32[2048,256]{0,1:T(8,128)S(1)} fusion(bf16[4,2048,256]{1,2,0:T(8,128)(2,1)} %all-to-all-done.2), kind=kLoop, calls=%fused_computation.32 | loop fusion | flops 3670016 | bytes 6291456 | tf_op jit(solution)/shard_map/reduce_sum | solution.py:20
  290.4 12.9 %all-to-all-start.3 = ((f32[64,1,257]{2,1,0:T(1,128)}), f32[64,1,257]{2,1,0:T(1,128)S(1)}, u32[]{:S(2)}, u32[]{:S(2)}) async-start(f32[64,1,257]{2,1,0:T(1,128)} %broadcast_in_dim.134), calls=%async_computation.3 | async-start | bytes 196608 | tf_op jit(solution)/shard_map/all_to_all | solution.py:25
  303.3 2.5 fusion.34
  308.1 5.8 %all-to-all-done.3 = f32[64,1,257]{2,1,0:T(1,128)S(1)} async-done(((f32[64,1,257]{2,1,0:T(1,128)}), f32[64,1,257]{2,1,0:T(1,128)S(1)}, u32[]{:S(2)}, u32[]{:S(2)}) %all-to-all-start.3) | async-done | bytes 65824 | tf_op jit(solution)/shard_map/all_to_all | solution.py:25
  (89 shorter events, 31.4 us)
Async XLA Ops:
  7.2 222.9 %copy-start = (bf16[256,1024]{1,0:T(8,128)(2,1)S(1)}, bf16[256,1024]{1,0:T(8,128)(2,1)}, u32[]{:S(2)}) copy-start(bf16[256,1024]{1,0:T(8,128)(2,1)} %param.19) | copy-start | bytes 1572868
  10.3 22.6 %all-to-all-start.1 = ((s32[64,2,1]{1,2,0:T(1,128)}), s32[64,2,1]{1,2,0:T(1,128)S(1)}, u32[]{:S(2)}, u32[]{:S(2)}) async-start(s32[64,2,1]{1,2,0:T(1,128)} %bitcast), calls=%async_computation.1 | async-start | bytes 65536 | tf_op jit(solution)/shard_map/all_to_all | solution.py:96
  26.6 41.1 %copy-start.4 = (s32[128]{0:T(128)S(1)}, s32[128]{0:T(128)}, u32[]{:S(2)}) copy-start(s32[128]{0:T(128)} %param.15) | copy-start | bytes 1540
  32.8 33.1 %all-to-all-start = ((bf16[64,32,256]{2,1,0:T(8,128)(2,1)}), bf16[64,32,256]{2,1,0:T(8,128)(2,1)S(1)}, u32[]{:S(2)}, u32[]{:S(2)}) async-start(bf16[64,32,256]{2,1,0:T(8,128)(2,1)} %bitcast.2), calls=%async_computation | async-start | bytes 2097152 | tf_op jit(solution)/shard_map/all_to_all | solution.py:102
  37.6 79.8 %all-gather.2.cloned.1.call-start = ((), (), s32[]{:S(2)}) async-start(), calls=%async_computation.4 | async-start | bytes 5242880 | tf_op jit(solution)/shard_map/all_gather | solution.py:106
  117.4 3.4 %copy-start.1 = (bf16[2048,1024]{1,0:T(8,128)(2,1)S(1)}, bf16[2048,1024]{1,0:T(8,128)(2,1)}, u32[]{:S(2)}) copy-start(bf16[2048,1024]{1,0:T(8,128)(2,1)} %all-gather.2.cloned.1.call-done) | copy-start | bytes 12582916
  122.2 1.1 copy-start.5
  123.4 2.3 copy-start.6
  125.7 2.3 copy-start.7
  233.4 5.7 %copy-start.2 = (bf16[128,16,256]{2,1,0:T(8,128)(2,1)S(1)}, bf16[128,16,256]{2,1,0:T(8,128)(2,1)}, u32[]{:S(2)}) copy-start(bf16[128,16,256]{2,1,0:T(8,128)(2,1)} %broadcast_select_fusion.1) | copy-start | bytes 3145732
  233.4 51.9 %all-to-all-start.2 = ((bf16[4,2048,256]{1,2,0:T(8,128)(2,1)}), bf16[4,2048,256]{1,2,0:T(8,128)(2,1)}, u32[]{:S(2)}, u32[]{:S(2)}) async-start(bf16[4,2048,256]{1,2,0:T(8,128)(2,1)} %bitcast.47), calls=%async_computation.2 | async-start | bytes 8388608 | tf_op jit(solution)/shard_map/all_to_all | solution.py:19
  285.3 3.3 %copy-start.3 = (bf16[2048,256]{0,1:T(8,128)(2,1)S(1)}, bf16[2048,256]{0,1:T(8,128)(2,1)}, u32[]{:S(2)}) copy-start(bf16[2048,256]{0,1:T(8,128)(2,1)} %copy.23) | copy-start | bytes 3145732
  290.4 23.5 %all-to-all-start.3 = ((f32[64,1,257]{2,1,0:T(1,128)}), f32[64,1,257]{2,1,0:T(1,128)S(1)}, u32[]{:S(2)}, u32[]{:S(2)}) async-start(f32[64,1,257]{2,1,0:T(1,128)} %broadcast_in_dim.134), calls=%async_computation.3 | async-start | bytes 196608 | tf_op jit(solution)/shard_map/all_to_all | solution.py:25
Sparse Core Ops, SparseCore 0:
  67.9 49.4 all-gather.1
where the time goes:
time: 323 us
  waiting for transfers between devices  133 us (41%)
  matrix products  99.3 us (31%)
  starting transfers between devices  35.8 us (11%)
  other arithmetic  22.8 us (7%)
  local copies, waits for them, and re-layouts  14.6 us (5%)
  between operations  14.3 us (4%)
    sub x4, matrix products, attend(): raised = jnp.where(allowed[None], jnp.exp(scores - peak), 0.0)  53.8 us
    all_gather x1, waiting for transfers between devices, on_device(): full_rows = lax.all_gather(own_cols, 'mp', axis=1, tiled=True)  49.4 us
    all_to_all x1, waiting for transfers between devices, sent_and_summed(): lax.all_to_all(cut_along(shard, dim, length), axis, 0, 0, tiled=True)  44.8 us
    dot_general x4, matrix products, attend(): jnp.einsum('hqk,khd->qhd', weights, values, preferred_element_type=jnp.fl...  34.9 us
    all_to_all x1, waiting for transfers between devices, on_device(): lax.all_to_all(outgoing, 'dp', split_axis=0, concat_axis=0, tiled=True)  26.7 us
    all_to_all x1, starting transfers between devices, on_device(): lax.all_to_all(slot_sent, 'dp', split_axis=0, concat_axis=0, tiled=True)  13.1 us
    all_to_all x1, starting transfers between devices, sent_to_all(): return lax.all_to_all(copies, axis, split_axis=0, concat_axis=0, tiled=True)  12.9 us
  transfers between devices with their start and end apart: 5, of which 5 were waited for; matrix products, arithmetic and copies ran while one was open for 4% of the time, Pallas kernels for 0%

commit v1 on v0

--- a/solution.py
+++ b/solution.py
@@ -1,3 +1,4 @@
+import functools
 import jax
 import jax.numpy as jnp
 from jax import lax
@@ -6,6 +7,14 @@
 HEAD_DIM = 64
 IMG_OWN = 16
 EPSILON = 1e-06
+
+
+def _expand_indices(x_in, where_dim):
+    part_next = lax.all_gather(x_in, axis_name="mp")
+    return jnp.concatenate(part_next, where_dim)
+
+
+convert_quotas = functools.partial(_expand_indices, where_dim=1)
 
 
 def cut_along(shard, dim, length):
@@ -103,7 +112,7 @@
     own_cols = jnp.take(
         incoming.reshape(slot_count, tile_size, part_width), arrive, axis=0
     ).reshape(slot_count * tile_size, part_width)
-    full_rows = lax.all_gather(own_cols, "mp", axis=1, tiled=True)
+    full_rows = convert_quotas(own_cols)
     count_rows = slot_count * tile_size
     segment = jnp.repeat(packed_image, tile_size)
     present = segment >= 0

time: 323 us -> 328 us (1.015)
  local copies, waits for them, and re-layouts: 14.6 us -> 22.5 us
  waiting for transfers between devices: 133 us -> 129 us
    all_gather x0 -> x1, local copies, waits for them, and re-layouts: none -> 6.39 us  [_expand_indices(): part_next = lax.all_gather(x_in, axis_name='mp')]
  transfers between devices with their start and end apart: 5 -> 5, of which waited for: 5 -> 5; matrix products, arithmetic and copies ran while one was open for 4% -> 5% of each run, Pallas kernels for 0% -> 0%
where the time goes in v1:
time: 328 us; the launch traced here: 327 us
  waiting for transfers between devices  129 us (39%)
  matrix products  99.4 us (30%)
  starting transfers between devices  34.6 us (11%)
  other arithmetic  24.9 us (8%)
  local copies, waits for them, and re-layouts  22.5 us (7%)
  between operations  14.3 us (4%)
    sub x4, matrix products, attend(): raised = jnp.where(allowed[None], jnp.exp(scores - peak), 0.0)  53.8 us
    all_gather x1, waiting for transfers between devices, _expand_indices(): part_next = lax.all_gather(x_in, axis_name='mp')  47.5 us
    all_to_all x1, waiting for transfers between devices, sent_and_summed(): lax.all_to_all(cut_along(shard, dim, length), axis, 0, 0, tiled=True)  42.9 us
    dot_general x4, matrix products, attend(): jnp.einsum('hqk,khd->qhd', weights, values, preferred_element_type=jnp.fl...  34.9 us
    all_to_all x1, waiting for transfers between devices, on_device(): lax.all_to_all(outgoing, 'dp', split_axis=0, concat_axis=0, tiled=True)  26.7 us
    all_to_all x1, starting transfers between devices, on_device(): lax.all_to_all(slot_sent, 'dp', split_axis=0, concat_axis=0, tiled=True)  13.1 us
    all_to_all x1, starting transfers between devices, sent_to_all(): return lax.all_to_all(copies, axis, split_axis=0, concat_axis=0, tiled=True)  11.7 us
  transfers between devices with their start and end apart: 5, of which 5 were waited for; matrix products, arithmetic and copies ran while one was open for 5% of the time, Pallas kernels for 0%

profile of v1, /device:TPU:1, one launch (start us, length us, event | category | flops | bytes accessed | tf_op | source)
XLA Modules:
  0.0 327.3 jit_solution(7081364711058602366)
XLA Ops:
  10.3 13.1 %all-to-all-start.1 = ((s32[64,2,1]{1,2,0:T(1,128)}), s32[64,2,1]{1,2,0:T(1,128)S(1)}, u32[]{:S(2)}, u32[]{:S(2)}) async-start(s32[64,2,1]{1,2,0:T(1,128)} %bitcast), calls=%async_computation.1 | async-start | bytes 65536 | tf_op jit(solution)/shard_map/all_to_all | solution.py:105
  26.6 6.2 %all-to-all-done.1 = s32[64,2,1]{1,2,0:T(1,128)S(1)} async-done(((s32[64,2,1]{1,2,0:T(1,128)}), s32[64,2,1]{1,2,0:T(1,128)S(1)}, u32[]{:S(2)}, u32[]{:S(2)}) %all-to-all-start.1) | async-done | bytes 544 | tf_op jit(solution)/shard_map/all_to_all | solution.py:105
  32.8 4.7 %all-to-all-start = ((bf16[64,32,256]{2,1,0:T(8,128)(2,1)}), bf16[64,32,256]{2,1,0:T(8,128)(2,1)S(1)}, u32[]{:S(2)}, u32[]{:S(2)}) async-start(bf16[64,32,256]{2,1,0:T(8,128)(2,1)} %bitcast.2), calls=%async_computation | async-start | bytes 2097152 | tf_op jit(solution)/shard_map/all_to_all | solution.py:111
  39.2 26.7 %all-to-all-done = bf16[64,32,256]{2,1,0:T(8,128)(2,1)S(1)} async-done(((bf16[64,32,256]{2,1,0:T(8,128)(2,1)}), bf16[64,32,256]{2,1,0:T(8,128)(2,1)S(1)}, u32[]{:S(2)}, u32[]{:S(2)}) %all-to-all-start) | async-done | bytes 1048608 | tf_op jit(solution)/shard_map/all_to_all | solution.py:111
  67.9 47.5 %all-gather.2.cloned.1.call-done = bf16[4,2048,256]{2,1,0:T(8,128)(2,1)} async-done(((bf16[1,2048,256]{2,1,0:T(8,128)(2,1)}), bf16[4,2048,256]{2,1,0:T(8,128)(2,1)}) %all-gather.2.cloned.1.call-update) | async-done | bytes 4194320 | tf_op jit(solution)/shard_map/all_gather | solution.py:13
  115.4 6.4 %copy.25 = bf16[4,2048,256]{1,2,0:T(8,128)(2,1)} copy(bf16[4,2048,256]{2,1,0:T(8,128)(2,1)} %all-gather.2.cloned.1.call-done) | data formatting | bytes 8388608 | tf_op jit(solution)/shard_map/all_gather | solution.py:13
  121.8 3.0 convert_reduce_fusion.1
  134.9 98.7 %while.11 = (s32[]{:T(128)}, bf16[4,512,4,64]{1,3,2,0:T(8,128)(2,1)S(1)}, s32[4]{0:T(128)S(1)}, s32[2048]{0:T(1024)S(1)}, pred[2048]{0:T(1024)(128)(4,1)S(1)}, /...) while((s32[]{:T(128)}, ...), condition=%wide.region_9.11_spmd.clone, body=%wide.region_6.0_spmd.clone.sunk | while | flops 1646399488 | bytes 40707776 | solution.py:84
  137.3 13.4 %fusion.63 = (f32[4,512]{1,0:T(4,128)S(1)}, f32[4,512,2048]{2,1,0:T(8,128)}) fusion(pred[512,2048]{1,0:T(8,128)(4,1)S(1)} %compare_and_fusion.4, bf16[2048,4,64]{0,2,1:T(8,128)(2,1)} %get-tuple-element.195, bf16[2048,4,64]{0,2,1:T(8,128)(2,1)} %get-tuple-element.194, s32[]{:T(128)S(6)} %select_n.102), kind=kOutput, calls=%fused_computation.72.clone.1 | convolution fusion | flops 1098909696 | bytes 21505024 | tf_op jit(solution)/shard_map/while/body/eval_jaxpr/sub | solution.py:63
  150.8 8.7 %fusion.64 = bf16[4,512,4,64]{1,3,2,0:T(8,128)(2,1)S(1)} fusion(bf16[4,512,4,64]{1,3,2,0:T(8,128)(2,1)S(1)} %get-tuple-element.177, s32[]{:T(128)} %get-tuple-element.176, bf16[2048,4,64]{0,2,1:T(8,128)(2,1)} %get-tuple-element.196, f32[4,512,2048]{2,1,0:T(8,128)} %get-tuple-element.161, f32[4,512]{1,0:T(4,128)S(1)} %broadcast_select_fusion.4), kind=kOutput, calls=%fused_computation.17.clone.1 | convolution fusion | flops 545390592 | bytes 18096132 | tf_op jit(solution)/shard_map/while/body/eval_jaxpr/hqk,khd->qhd/dot_general | solution.py:67
  162.0 13.4 %fusion.63 = (f32[4,512]{1,0:T(4,128)S(1)}, f32[4,512,2048]{2,1,0:T(8,128)}) fusion(pred[512,2048]{1,0:T(8,128)(4,1)S(1)} %compare_and_fusion.4, bf16[2048,4,64]{0,2,1:T(8,128)(2,1)} %get-tuple-element.195, bf16[2048,4,64]{0,2,1:T(8,128)(2,1)} %get-tuple-element.194, s32[]{:T(128)S(6)} %select_n.102), kind=kOutput, calls=%fused_computation.72.clone.1 | convolution fusion | flops 1098909696 | bytes 21505024 | tf_op jit(solution)/shard_map/while/body/eval_jaxpr/sub | solution.py:63
  175.4 8.7 %fusion.64 = bf16[4,512,4,64]{1,3,2,0:T(8,128)(2,1)S(1)} fusion(bf16[4,512,4,64]{1,3,2,0:T(8,128)(2,1)S(1)} %get-tuple-element.177, s32[]{:T(128)} %get-tuple-element.176, bf16[2048,4,64]{0,2,1:T(8,128)(2,1)} %get-tuple-element.196, f32[4,512,2048]{2,1,0:T(8,128)} %get-tuple-element.161, f32[4,512]{1,0:T(4,128)S(1)} %broadcast_select_fusion.4), kind=kOutput, calls=%fused_computation.17.clone.1 | convolution fusion | flops 545390592 | bytes 18096132 | tf_op jit(solution)/shard_map/while/body/eval_jaxpr/hqk,khd->qhd/dot_general | solution.py:67
  186.6 13.5 %fusion.63 = (f32[4,512]{1,0:T(4,128)S(1)}, f32[4,512,2048]{2,1,0:T(8,128)}) fusion(pred[512,2048]{1,0:T(8,128)(4,1)S(1)} %compare_and_fusion.4, bf16[2048,4,64]{0,2,1:T(8,128)(2,1)} %get-tuple-element.195, bf16[2048,4,64]{0,2,1:T(8,128)(2,1)} %get-tuple-element.194, s32[]{:T(128)S(6)} %select_n.102), kind=kOutput, calls=%fused_computation.72.clone.1 | convolution fusion | flops 1098909696 | bytes 21505024 | tf_op jit(solution)/shard_map/while/body/eval_jaxpr/sub | solution.py:63
  200.1 8.7 %fusion.64 = bf16[4,512,4,64]{1,3,2,0:T(8,128)(2,1)S(1)} fusion(bf16[4,512,4,64]{1,3,2,0:T(8,128)(2,1)S(1)} %get-tuple-element.177, s32[]{:T(128)} %get-tuple-element.176, bf16[2048,4,64]{0,2,1:T(8,128)(2,1)} %get-tuple-element.196, f32[4,512,2048]{2,1,0:T(8,128)} %get-tuple-element.161, f32[4,512]{1,0:T(4,128)S(1)} %broadcast_select_fusion.4), kind=kOutput, calls=%fused_computation.17.clone.1 | convolution fusion | flops 545390592 | bytes 18096132 | tf_op jit(solution)/shard_map/while/body/eval_jaxpr/hqk,khd->qhd/dot_general | solution.py:67
  211.4 13.4 %fusion.63 = (f32[4,512]{1,0:T(4,128)S(1)}, f32[4,512,2048]{2,1,0:T(8,128)}) fusion(pred[512,2048]{1,0:T(8,128)(4,1)S(1)} %compare_and_fusion.4, bf16[2048,4,64]{0,2,1:T(8,128)(2,1)} %get-tuple-element.195, bf16[2048,4,64]{0,2,1:T(8,128)(2,1)} %get-tuple-element.194, s32[]{:T(128)S(6)} %select_n.102), kind=kOutput, calls=%fused_computation.72.clone.1 | convolution fusion | flops 1098909696 | bytes 21505024 | tf_op jit(solution)/shard_map/while/body/eval_jaxpr/sub | solution.py:63
  224.8 8.7 %fusion.64 = bf16[4,512,4,64]{1,3,2,0:T(8,128)(2,1)S(1)} fusion(bf16[4,512,4,64]{1,3,2,0:T(8,128)(2,1)S(1)} %get-tuple-element.177, s32[]{:T(128)} %get-tuple-element.176, bf16[2048,4,64]{0,2,1:T(8,128)(2,1)} %get-tuple-element.196, f32[4,512,2048]{2,1,0:T(8,128)} %get-tuple-element.161, f32[4,512]{1,0:T(4,128)S(1)} %broadcast_select_fusion.4), kind=kOutput, calls=%fused_computation.17.clone.1 | convolution fusion | flops 545390592 | bytes 18096132 | tf_op jit(solution)/shard_map/while/body/eval_jaxpr/hqk,khd->qhd/dot_general | solution.py:67
  234.6 3.3 %convolution_convert_fusion = bf16[2048,1024]{0,1:T(8,128)(2,1)} fusion(bf16[2048,256]{0,1:T(8,128)(2,1)S(1)} %bitcast.60, bf16[256,1024]{1,0:T(8,128)(2,1)S(1)} %copy-done), kind=kOutput, calls=%fused_computation.32 | convolution fusion | flops 1075838976 | bytes 5767168 | tf_op jit(solution)/shard_map/dot_general | solution.py:137
  237.9 5.0 %all-to-all-start.2 = ((bf16[4,2048,256]{1,2,0:T(8,128)(2,1)}), bf16[4,2048,256]{1,2,0:T(8,128)(2,1)}, u32[]{:S(2)}, u32[]{:S(2)}) async-start(bf16[4,2048,256]{1,2,0:T(8,128)(2,1)} %bitcast.58), calls=%async_computation.2 | async-start | bytes 8388608 | tf_op jit(solution)/shard_map/all_to_all | solution.py:28
  245.2 3.0 copy.27
  248.1 42.9 %all-to-all-done.2 = bf16[4,2048,256]{1,2,0:T(8,128)(2,1)} async-done(((bf16[4,2048,256]{1,2,0:T(8,128)(2,1)}), bf16[4,2048,256]{1,2,0:T(8,128)(2,1)}, u32[]{:S(2)}, u32[]{:S(2)}) %all-to-all-start.2) | async-done | bytes 4194336 | tf_op jit(solution)/shard_map/all_to_all | solution.py:28
  291.0 3.3 %convert_reduce_fusion = f32[2048,256]{0,1:T(8,128)S(1)} fusion(bf16[4,2048,256]{1,2,0:T(8,128)(2,1)} %all-to-all-done.2), kind=kLoop, calls=%fused_computation.29 | loop fusion | flops 3670016 | bytes 6291456 | tf_op jit(solution)/shard_map/reduce_sum | solution.py:29
  296.2 11.7 %all-to-all-start.3 = ((f32[64,1,257]{2,1,0:T(1,128)}), f32[64,1,257]{2,1,0:T(1,128)S(1)}, u32[]{:S(2)}, u32[]{:S(2)}) async-start(f32[64,1,257]{2,1,0:T(1,128)} %broadcast_in_dim.134), calls=%async_computation.3 | async-start | bytes 196608 | tf_op jit(solution)/shard_map/all_to_all | solution.py:34
  307.9 3.0 fusion.31
  313.2 5.4 %all-to-all-done.3 = f32[64,1,257]{2,1,0:T(1,128)S(1)} async-done(((f32[64,1,257]{2,1,0:T(1,128)}), f32[64,1,257]{2,1,0:T(1,128)S(1)}, u32[]{:S(2)}, u32[]{:S(2)}) %all-to-all-start.3) | async-done | bytes 65824 | tf_op jit(solution)/shard_map/all_to_all | solution.py:34
  (91 shorter events, 36.3 us)
Async XLA Ops:
  7.2 227.5 %copy-start = (bf16[256,1024]{1,0:T(8,128)(2,1)S(1)}, bf16[256,1024]{1,0:T(8,128)(2,1)}, u32[]{:S(2)}) copy-start(bf16[256,1024]{1,0:T(8,128)(2,1)} %param.19) | copy-start | bytes 1572868
  10.3 22.6 %all-to-all-start.1 = ((s32[64,2,1]{1,2,0:T(1,128)}), s32[64,2,1]{1,2,0:T(1,128)S(1)}, u32[]{:S(2)}, u32[]{:S(2)}) async-start(s32[64,2,1]{1,2,0:T(1,128)} %bitcast), calls=%async_computation.1 | async-start | bytes 65536 | tf_op jit(solution)/shard_map/all_to_all | solution.py:105
  26.6 41.1 %copy-start.4 = (s32[128]{0:T(128)S(1)}, s32[128]{0:T(128)}, u32[]{:S(2)}) copy-start(s32[128]{0:T(128)} %param.15) | copy-start | bytes 1540
  32.8 33.1 %all-to-all-start = ((bf16[64,32,256]{2,1,0:T(8,128)(2,1)}), bf16[64,32,256]{2,1,0:T(8,128)(2,1)S(1)}, u32[]{:S(2)}, u32[]{:S(2)}) async-start(bf16[64,32,256]{2,1,0:T(8,128)(2,1)} %bitcast.2), calls=%async_computation | async-start | bytes 2097152 | tf_op jit(solution)/shard_map/all_to_all | solution.py:111
  37.6 77.8 %all-gather.2.cloned.1.call-start = ((), (), s32[]{:S(2)}) async-start(), calls=%async_computation.4 | async-start | bytes 5242880 | tf_op jit(solution)/shard_map/all_gather | solution.py:13
  121.8 3.4 %copy-start.1 = (bf16[4,2048,256]{1,2,0:T(8,128)(2,1)S(1)}, bf16[4,2048,256]{1,2,0:T(8,128)(2,1)}, u32[]{:S(2)}) copy-start(bf16[4,2048,256]{1,2,0:T(8,128)(2,1)} %copy.25) | copy-start | bytes 12582916
  126.4 1.5 copy-start.5
  127.9 2.3 copy-start.6
  130.2 2.3 copy-start.7
  237.9 5.7 %copy-start.3 = (bf16[128,16,256]{2,1,0:T(8,128)(2,1)S(1)}, bf16[128,16,256]{2,1,0:T(8,128)(2,1)}, u32[]{:S(2)}) copy-start(bf16[128,16,256]{2,1,0:T(8,128)(2,1)} %broadcast_select_fusion.1) | copy-start | bytes 3145732
  237.9 53.1 %all-to-all-start.2 = ((bf16[4,2048,256]{1,2,0:T(8,128)(2,1)}), bf16[4,2048,256]{1,2,0:T(8,128)(2,1)}, u32[]{:S(2)}, u32[]{:S(2)}) async-start(bf16[4,2048,256]{1,2,0:T(8,128)(2,1)} %bitcast.58), calls=%async_computation.2 | async-start | bytes 8388608 | tf_op jit(solution)/shard_map/all_to_all | solution.py:28
  291.0 3.3 %copy-start.2 = (f32[2048,256]{0,1:T(8,128)S(1)}, f32[2048,256]{0,1:T(8,128)}, u32[]{:S(2)}) copy-start(f32[2048,256]{0,1:T(8,128)} %copy.27) | copy-start | bytes 6291460
  296.2 22.3 %all-to-all-start.3 = ((f32[64,1,257]{2,1,0:T(1,128)}), f32[64,1,257]{2,1,0:T(1,128)S(1)}, u32[]{:S(2)}, u32[]{:S(2)}) async-start(f32[64,1,257]{2,1,0:T(1,128)} %broadcast_in_dim.134), calls=%async_computation.3 | async-start | bytes 196608 | tf_op jit(solution)/shard_map/all_to_all | solution.py:34
Sparse Core Ops, SparseCore 0:
  67.9 47.4 all-gather.1
